TPU v7x, 64 devices: a 2x2x8 block of a 4x4x8 slice. The times are simulated.
64 devices in a mesh: batch: 4 (over x, y), tree: 16 (over z, core).
Axes of the slice: x: 2, y: 2, z: 8, core: 2. Of those that a mesh axis runs over, the one named last changes fastest.
The devices are a block of a 4x4x8 slice.
Arguments:
- x_vecs: float32 [262144, 512], P(('batch', 'tree')), parts along dimension 0
- d_near: bfloat16 [128, 512, 512], P('tree')
- u_leaf: bfloat16 [128, 512, 128], P('tree')
- v_leaf: bfloat16 [128, 512, 128], P('tree')
- w_h0: bfloat16 [128, 128, 256], P('tree')
- r_h0: bfloat16 [128, 128, 256], P('tree')
- b_h0: bfloat16 [128, 128, 128], P('tree')
- w_h1: bfloat16 [64, 256, 256], P('tree')
- r_h1: bfloat16 [64, 256, 256], P('tree')
- b_h1: bfloat16 [64, 256, 256], P('tree')
- w_h2: bfloat16 [32, 256, 512], P('tree')
- r_h2: bfloat16 [32, 256, 512], P('tree')
- b_h2: bfloat16 [32, 256, 256], P('tree')
- w_upper: bfloat16 [16, 512, 512], P('tree')
- r_upper: bfloat16 [16, 512, 512], P('tree')
- b_upper: bfloat16 [16, 512, 512], P('tree')
- w_top: bfloat16 [12, 512, 512], replicated
- r_top: bfloat16 [12, 512, 512], replicated
- b_top: bfloat16 [14, 512, 512], replicated
Outputs:
- output: float32 [262144, 512], P(('batch', 'tree')), parts along dimension 0
There are 4 independent parts. A program takes and returns all parts, laid end to end along the dimension named above; an argument that names none is the same for every part.
All inputs are finite; a program needn't handle non-finite values.
Results may differ from a plain program's by a relative error of at most 0.0116554.
Values are sent between devices in bfloat16 or wider.
A program may use at most 768 MiB of HBM per device.

v0:
```python
import math
import jax
import jax.numpy as jnp
from jax import lax
from jax.sharding import PartitionSpec as P


def log_two(count):
    return int(math.log2(count) + 0.5)


def local_blocks(packed):
    depth = log_two(packed.shape[0] + 1)
    return [packed[2 ** step - 1:2 ** (step + 1) - 1] for step in range(depth)]


def merge_local(w_child, x_child):
    prod = jnp.einsum('nkq,nkc->nqc', w_child, x_child, preferred_element_type=jnp.float32)
    pairs = prod.reshape(prod.shape[0] // 2, 2, prod.shape[1], prod.shape[2])
    return (pairs[:, 0] + pairs[:, 1]).astype(jnp.bfloat16)


def couple_local(b_node, x_level):
    pairs = x_level.reshape(x_level.shape[0] // 2, 2, x_level.shape[1], x_level.shape[2])
    swapped = jnp.flip(pairs, axis=1).reshape(x_level.shape)
    return jnp.einsum('nkj,njc->nkc', b_node, swapped, preferred_element_type=jnp.float32)


def push_local(r_child, y_parent, coupled):
    r_pairs = r_child.reshape(r_child.shape[0] // 2, 2, r_child.shape[1], r_child.shape[2])
    prod = jnp.einsum('nekq,nqc->nekc', r_pairs, y_parent, preferred_element_type=jnp.float32)
    return (coupled + prod.reshape(coupled.shape)).astype(jnp.bfloat16)


def pick_node(table, index):
    return lax.dynamic_index_in_dim(table, index, 0, keepdims=False)


def solution(mesh):
    tree_devs = mesh.shape['tree']
    top_depth = log_two(tree_devs)
    rows_spec = P(('batch', 'tree'), None)
    tree_spec = P('tree', None, None)
    full_spec = P(None, None, None)

    def body(x_loc, d_near, u_leaf, v_leaf, w_h0, r_h0, b_h0, w_h1, r_h1, b_h1, w_h2, r_h2, b_h2, w_upper, r_upper, b_upper, w_top, r_top, b_top):
        my_dev = lax.axis_index('tree')
        leaves_dev, leaf_size, leaf_rank = u_leaf.shape
        rhs_cols = x_loc.shape[1]
        x_leaf = x_loc.astype(jnp.bfloat16).reshape(leaves_dev, leaf_size, rhs_cols)
        blocks_w = local_blocks(w_upper)
        blocks_r = local_blocks(r_upper)
        blocks_b = local_blocks(b_upper)
        w_local = [w_h0, w_h1, w_h2] + list(reversed(blocks_w[1:]))
        r_local = [r_h0, r_h1, r_h2] + list(reversed(blocks_r[1:]))
        b_local = [b_h0, b_h1, b_h2] + list(reversed(blocks_b[1:]))
        skel_up = [jnp.einsum('lmk,lmc->lkc', v_leaf, x_leaf, preferred_element_type=jnp.float32).astype(jnp.bfloat16)]
        for w_child in w_local:
            skel_up.append(merge_local(w_child, skel_up[-1]))
        coupled = [couple_local(b_node, x_level) for b_node, x_level in zip(b_local, skel_up[:-1])]
        node_x = skel_up[-1][0]
        own_part = jnp.einsum('kq,kc->qc', blocks_w[0][0], node_x, preferred_element_type=jnp.float32)
        node_idx = my_dev
        step_coupled = []
        for step in range(top_depth):
            stride = 2 ** step
            level = top_depth - step
            pair_list = [(source, source ^ stride) for source in range(tree_devs)]
            sib_x = lax.ppermute(node_x, 'tree', pair_list)
            if step == 0:
                b_here = blocks_b[0][0]
            else:
                b_here = pick_node(b_top, 2 ** level - 2 + node_idx)
            step_coupled.append(jnp.dot(b_here, sib_x, preferred_element_type=jnp.float32))
            if level > 1:
                if step == 0:
                    mine = own_part
                    theirs = lax.ppermute(own_part, 'tree', pair_list)
                else:
                    sib_idx = node_idx + 1 - 2 * (node_idx % 2)
                    mine = jnp.einsum('kq,kc->qc', pick_node(w_top, 2 ** level - 4 + node_idx), node_x, preferred_element_type=jnp.float32)
                    theirs = jnp.einsum('kq,kc->qc', pick_node(w_top, 2 ** level - 4 + sib_idx), sib_x, preferred_element_type=jnp.float32)
                node_x = (mine + theirs).astype(jnp.bfloat16)
                node_idx = node_idx // 2
        y_node = step_coupled[-1].astype(jnp.bfloat16)
        for step in range(top_depth - 2, -1, -1):
            level = top_depth - step
            if step == 0:
                r_here = blocks_r[0][0]
            else:
                r_here = pick_node(r_top, 2 ** level - 4 + my_dev // 2 ** step)
            y_node = (step_coupled[step] + jnp.dot(r_here, y_node, preferred_element_type=jnp.float32)).astype(jnp.bfloat16)
        y_skel = y_node[None]
        for height in range(len(r_local) - 1, -1, -1):
            y_skel = push_local(r_local[height], y_skel, coupled[height])
        near = jnp.einsum('lmj,ljc->lmc', d_near, x_leaf, preferred_element_type=jnp.float32)
        far = jnp.einsum('lmk,lkc->lmc', u_leaf, y_skel, preferred_element_type=jnp.float32)
        return (near + far).reshape(leaves_dev * leaf_size, rhs_cols)

    return jax.shard_map(body, mesh=mesh, in_specs=(rows_spec,) + (tree_spec,) * 15 + (full_spec,) * 3, out_specs=rows_spec, check_vma=False)
```

profile of v0, /device:TPU:21, one launch (start us, length us, event | category | flops | bytes accessed | tf_op | source)
XLA Modules:
  0.0 116.5 jit_solution(18084405080567755538)
XLA Ops:
  0.0 4.1 %convert_element_type.63 = bf16[4096,512]{1,0:T(8,128)(2,1)S(1)} convert(f32[4096,512]{1,0:T(8,128)} %param.19) | non-fusion elementwise | flops 2097152 | bytes 12582912 | tf_op jit(solution)/shard_map/convert_element_type | solution.py:50
  4.1 0.8 convolution_convert_fusion
  5.0 0.5 copy-done.13
  5.5 0.8 fusion.65
  7.3 0.5 copy-done.11
  8.2 1.0 fusion.24
  9.2 1.5 %convolution_bitcast_fusion.2 = f32[512,512]{0,1:T(8,128)S(1)} fusion(bf16[512,512]{0,1:T(8,128)(2,1)} %fusion.24, bf16[1,512,512]{2,1,0:T(8,128)(2,1)S(1)} %copy-done.12), kind=kOutput, calls=%fused_computation.18 | convolution fusion | flops 268435456 | bytes 2097152 | tf_op jit(solution)/shard_map/kq,kc->qc/dot_general | solution.py:62
  10.6 4.8 %collective-permute-start.1 = (f32[512,512]{0,1:T(8,128)S(1)}, f32[512,512]{0,1:T(8,128)S(1)}, u32[]{:S(2)}, u32[]{:S(2)}) collective-permute-start(f32[512,512]{0,1:T(8,128)S(1)} %convolution_bitcast_fusion.2), channel_id=1, source_target_pairs={{0,1},{1,0},{2,3},{3,2},{4,5},{5,4},{6,7},{7,6},{8,9},{9,8},{10,11... | collective-permute-start | bytes 3145736 | tf_op jit(solution)/shard_map/ppermute | solution.py:78
  15.4 2.3 %collective-permute-done.1 = f32[512,512]{0,1:T(8,128)S(1)} collective-permute-done((f32[512,512]{0,1:T(8,128)S(1)}, f32[512,512]{0,1:T(8,128)S(1)}, u32[]{:S(2)}, u32[]{:S(2)}) %collective-permute-start.1) | collective-permute-done | bytes 1048608 | tf_op jit(solution)/shard_map/ppermute | solution.py:78
  17.7 1.0 add_convert_fusion
  19.0 1.9 %reshape.76 = bf16[2,256,512]{1,2,0:T(8,128)(2,1)} reverse(bf16[2,256,512]{1,2,0:T(8,128)(2,1)} %copy-done.4), dimensions={0} | reverse | bytes 1048576 | tf_op jit(solution)/shard_map/reshape | solution.py:25
  20.9 1.0 rev.10
  22.0 1.1 rev.11
  23.1 8.8 %collective-permute-done.2 = bf16[512,512]{0,1:T(8,128)(2,1)} collective-permute-done((bf16[512,512]{0,1:T(8,128)(2,1)}, bf16[512,512]{0,1:T(8,128)(2,1)}, u32[]{:S(2)}, u32[]{:S(2)}) %collective-permute-start.2) | collective-permute-done | bytes 524320 | tf_op jit(solution)/shard_map/ppermute | solution.py:69
  31.9 1.7 %fusion.32 = f32[512,512]{1,0:T(8,128)S(1)} fusion(bf16[512,512]{0,1:T(8,128)(2,1)} %collective-permute-done.2, bf16[12,512,512]{2,1,0:T(8,128)(2,1)} %param.35, s32[]{:T(128)S(6)} %select_n.58), kind=kOutput, calls=%fused_computation.51 | convolution fusion | flops 268435456 | bytes 2097156 | tf_op jit(solution)/shard_map/kq,kc->qc/dot_general | solution.py:82
  33.6 1.8 %fusion.8 = bf16[512,512]{1,0:T(8,128)(2,1)S(1)} fusion(f32[512,512]{1,0:T(8,128)S(1)} %fusion.32, bf16[512,512]{0,1:T(8,128)(2,1)} %add_convert_fusion, bf16[12,512,512]{2,1,0:T(8,128)(2,1)} %param.35, s32[]{:T(128)S(6)} %select_n.54), kind=kOutput, calls=%fused_computation.24 | convolution fusion | flops 268959744 | bytes 2621444 | tf_op jit(solution)/shard_map/kq,kc->qc/dot_general | solution.py:81
  35.4 0.9 collective-permute-start.3
  36.4 1.3 %convolution_bitcast_fusion.3 = f32[2,256,512]{1,2,0:T(8,128)} fusion(bf16[2,256,512]{1,2,0:T(8,128)(2,1)S(1)} %copy-done.5, bf16[2,256,256]{2,1,0:T(8,128)(2,1)S(1)} %copy-done.14), kind=kOutput, calls=%fused_computation.20 | convolution fusion | flops 134217728 | bytes 1835008 | tf_op jit(solution)/shard_map/nkj,njc->nkc/dot_general | solution.py:26
  37.7 1.5 %fusion.27 = f32[512,512]{1,0:T(8,128)S(1)} fusion(bf16[512,512]{1,0:T(8,128)(2,1)S(1)} %fusion.8, bf16[12,512,512]{2,1,0:T(8,128)(2,1)} %param.35, s32[]{:T(128)S(6)} %select_n.63), kind=kOutput, calls=%fused_computation.47 | convolution fusion | flops 268435456 | bytes 2097156 | tf_op jit(solution)/shard_map/kq,kc->qc/dot_general | solution.py:81
  39.2 22.0 %collective-permute-done.3 = bf16[512,512]{1,0:T(8,128)(2,1)S(1)} collective-permute-done((bf16[512,512]{1,0:T(8,128)(2,1)S(1)}, bf16[512,512]{1,0:T(8,128)(2,1)S(1)}, u32[]{:S(2)}, u32[]{:S(2)}) %collective-permute-start.3) | collective-permute-done | bytes 524320 | tf_op jit(solution)/shard_map/ppermute | solution.py:69
  61.2 1.7 %fusion.10 = bf16[512,512]{1,0:T(8,128)(2,1)S(1)} fusion(f32[512,512]{1,0:T(8,128)S(1)} %fusion.27, bf16[512,512]{1,0:T(8,128)(2,1)S(1)} %collective-permute-done.3, bf16[12,512,512]{2,1,0:T(8,128)(2,1)} %param.35, s32[]{:T(128)S(6)} %select_n.65), kind=kOutput, calls=%fused_computation.26 | convolution fusion | flops 268959744 | bytes 2621444 | tf_op jit(solution)/shard_map/kq,kc->qc/dot_general | solution.py:82
  62.9 4.4 %collective-permute-start.4 = (bf16[512,512]{1,0:T(8,128)(2,1)S(1)}, bf16[512,512]{1,0:T(8,128)(2,1)S(1)}, u32[]{:S(2)}, u32[]{:S(2)}) collective-permute-start(bf16[512,512]{1,0:T(8,128)(2,1)S(1)} %fusion.10), channel_id=1, source_target_pairs={{0,8},{1,9},{2,10},{3,11},{4,12},{5,13},{6,14},{7,15},{8,0},{9,1},... | collective-permute-start | bytes 1572872 | tf_op jit(solution)/shard_map/ppermute | solution.py:69
  67.3 5.7 %fusion.64 = f32[8,512,512]{2,1,0:T(8,128)} fusion(bf16[8,512,512]{2,1,0:T(8,128)(2,1)S(1)} %copy-done.3, bf16[8,512,512]{2,1,0:T(8,128)(2,1)S(1)} %bitcast.168), kind=kOutput, calls=%fused_computation.75 | convolution fusion | flops 2147483648 | bytes 16777216 | tf_op jit(solution)/shard_map/lmj,ljc->lmc/dot_general | solution.py:96
  73.1 17.5 %collective-permute-done.4 = bf16[512,512]{1,0:T(8,128)(2,1)S(1)} collective-permute-done((bf16[512,512]{1,0:T(8,128)(2,1)S(1)}, bf16[512,512]{1,0:T(8,128)(2,1)S(1)}, u32[]{:S(2)}, u32[]{:S(2)}) %collective-permute-start.4) | collective-permute-done | bytes 524320 | tf_op jit(solution)/shard_map/ppermute | solution.py:69
  90.6 3.0 %fusion.14 = f32[512,512]{1,0:T(8,128)} fusion(bf16[512,512]{1,0:T(8,128)(2,1)S(1)} %collective-permute-done.4, bf16[14,512,512]{2,1,0:T(8,128)(2,1)} %param.37, s32[]{:T(128)S(6)} %select_n.62, bf16[12,512,512]{2,1,0:T(8,128)(2,1)} %param.36, s32[]{:T(128)S(6)} %select_n.60), kind=kOutput, calls=%fused_computation.30 | convolution fusion | flops 537133056 | bytes 2621448 | tf_op jit(solution)/shard_map/dot_general | solution.py:92
  93.5 2.3 %fusion.15 = f32[512,512]{1,0:T(8,128)S(1)} fusion(f32[512,512]{1,0:T(8,128)} %fusion.14, bf16[512,512]{1,0:T(8,128)(2,1)S(1)} %copy-done.7, bf16[14,512,512]{2,1,0:T(8,128)(2,1)} %param.37, s32[]{:T(128)S(6)} %select_n.56, bf16[12,512,512]{2,1,0:T(8,128)(2,1)} %param.36, s32[]{:T(128)S(6)} %select_n.54), kind=kOutput, calls=%fused_computation.31 | convolution fusion | flops 537395200 | bytes 3670024 | tf_op jit(solution)/shard_map/dot_general | solution.py:92
  95.9 2.2 %fusion.16 = f32[512,512]{1,0:T(8,128)S(1)} fusion(f32[512,512]{1,0:T(8,128)S(1)} %fusion.15, bf16[512,512]{0,1:T(8,128)(2,1)} %collective-permute-done.2, bf16[1,512,512]{2,1,0:T(8,128)(2,1)} %param.33, bf16[14,512,512]{2,1,0:T(8,128)(2,1)} %param.37, s32[]{:T(128)S(6)} %select_n.53), kind=kOutput, calls=%fused_computation.32 | convolution fusion | flops 537395200 | bytes 3670020 | tf_op jit(solution)/shard_map/dot_general | solution.py:92
  98.1 2.5 %fusion.13 = bf16[512,512,1]{1,0,2:T(8,128)(2,1)} fusion(f32[512,512]{1,0:T(8,128)S(1)} %fusion.16, bf16[512,512]{0,1:T(8,128)(2,1)} %collective-permute-done, bf16[1,512,512]{2,1,0:T(8,128)(2,1)} %param.34), kind=kOutput, calls=%fused_computation.29 | convolution fusion | flops 268959744 | bytes 2621440 | tf_op jit(solution)/shard_map/dot_general | solution.py:74
  100.6 2.4 %fusion.22 = f32[2,512,2,256]{3,1,2,0:T(8,128)S(1)} fusion(bf16[2,2,256,256]{3,2,1,0:T(8,128)(2,1)} %bitcast.176, f32[2,256,512]{1,2,0:T(8,128)} %convolution_bitcast_fusion.3, bf16[512,512,1]{1,0,2:T(8,128)(2,1)} %fusion.13, bf16[2,256,512]{2,1,0:T(8,128)(2,1)} %param.30), kind=kOutput, calls=%fused_computation.42 | convolution fusion | flops 537395200 | bytes 4718592 | tf_op jit(solution)/shard_map/nekq,nqc->nekc/dot_general | solution.py:31
  103.0 1.9 %fusion.4 = bf16[4,256,512,1]{1,2,3,0:T(8,128)(2,1)S(1)} fusion(f32[2,512,2,256]{3,1,2,0:T(8,128)S(1)} %fusion.22, bf16[4,256,512]{1,2,0:T(8,128)(2,1)} %bitcast.174, bf16[4,256,256]{2,1,0:T(8,128)(2,1)} %param.28), kind=kOutput, calls=%fused_computation.11 | convolution fusion | flops 269484032 | bytes 4718592 | tf_op jit(solution)/shard_map/nkj,njc->nkc/dot_general | solution.py:26
  105.4 1.8 %copy.26 = f32[8,128,512]{2,1,0:T(8,128)} copy(f32[8,128,512]{1,2,0:T(8,128)S(1)} %bitcast.173) | data formatting | bytes 4194304 | tf_op jit(solution)/shard_map/reshape | solution.py:32
  107.2 9.3 %bitcast_add_fusion = f32[8,512,512]{2,1,0:T(8,128)} fusion(f32[8,512,512]{2,1,0:T(8,128)} %fusion.64, bf16[8,512,128]{2,1,0:T(8,128)(2,1)S(1)} %copy-done, f32[8,128,512]{2,1,0:T(8,128)} %copy.26, bf16[8,128,128]{2,1,0:T(8,128)(2,1)S(1)} %copy-done.15, bf16[8,128,512]{2,1,0:T(8,128)(2,1)} %bitcast.175), kind=kOutput, calls=%fused_computation | convolution fusion | flops 674234368 | bytes 21233664 | tf_op jit(solution)/shard_map/lmk,lkc->lmc/dot_general | solution.py:97
  (38 shorter events, 2.3 us)
Async XLA Ops:
  0.0 107.2 %copy-start = (bf16[8,512,128]{2,1,0:T(8,128)(2,1)S(1)}, bf16[8,512,128]{2,1,0:T(8,128)(2,1)}, u32[]{:S(2)}) copy-start(bf16[8,512,128]{2,1,0:T(8,128)(2,1)} %param.21) | copy-start | bytes 3145732
  0.0 4.1 %copy-start.8 = (bf16[8,512,128]{2,1,0:T(8,128)(2,1)S(1)}, bf16[8,512,128]{2,1,0:T(8,128)(2,1)}, u32[]{:S(2)}) copy-start(bf16[8,512,128]{2,1,0:T(8,128)(2,1)} %param.22) | copy-start | bytes 3145732
  4.1 2.2 %copy-start.1 = (bf16[4096,512]{1,0:T(8,128)(2,1)}, bf16[4096,512]{1,0:T(8,128)(2,1)S(1)}, u32[]{:S(2)}) copy-start(bf16[4096,512]{1,0:T(8,128)(2,1)S(1)} %convert_element_type.63) | copy-start | bytes 12582916
  4.1 1.4 %copy-start.13 = (bf16[8,128,256]{2,1,0:T(8,128)(2,1)S(1)}, bf16[8,128,256]{2,1,0:T(8,128)(2,1)}, u32[]{:S(2)}) copy-start(bf16[8,128,256]{2,1,0:T(8,128)(2,1)} %param.23) | copy-start | bytes 1572868
  5.5 1.2 %copy-start.9 = (bf16[4,256,256]{2,1,0:T(8,128)(2,1)S(1)}, bf16[4,256,256]{2,1,0:T(8,128)(2,1)}, u32[]{:S(2)}) copy-start(bf16[4,256,256]{2,1,0:T(8,128)(2,1)} %param.26) | copy-start | bytes 1572868
  6.7 1.0 copy-start.11
  7.2 2.0 %copy-start.12 = (bf16[1,512,512]{2,1,0:T(8,128)(2,1)S(1)}, bf16[1,512,512]{2,1,0:T(8,128)(2,1)}, u32[]{:S(2)}) copy-start(bf16[1,512,512]{2,1,0:T(8,128)(2,1)} %param.32) | copy-start | bytes 1572868
  7.8 10.9 %copy-start.4 = (bf16[2,256,512]{1,2,0:T(8,128)(2,1)}, bf16[2,256,512]{1,2,0:T(8,128)(2,1)S(1)}, u32[]{:S(2)}) copy-start(bf16[2,256,512]{1,2,0:T(8,128)(2,1)S(1)} %fusion.23) | copy-start | bytes 1572868
  10.6 7.1 %collective-permute-start.1 = (f32[512,512]{0,1:T(8,128)S(1)}, f32[512,512]{0,1:T(8,128)S(1)}, u32[]{:S(2)}, u32[]{:S(2)}) collective-permute-start(f32[512,512]{0,1:T(8,128)S(1)} %convolution_bitcast_fusion.2), channel_id=1, source_target_pairs={{0,1},{1,0},{2,3},{3,2},{4,5},{5,4},{6,7},{7,6},{8,9},{9,8},{10,11... | collective-permute-start | bytes 3145736 | tf_op jit(solution)/shard_map/ppermute | solution.py:78
  18.7 13.2 %collective-permute-start.2 = (bf16[512,512]{0,1:T(8,128)(2,1)}, bf16[512,512]{0,1:T(8,128)(2,1)}, u32[]{:S(2)}, u32[]{:S(2)}) collective-permute-start(bf16[512,512]{0,1:T(8,128)(2,1)} %add_convert_fusion), channel_id=1, source_target_pairs={{0,2},{1,3},{2,0},{3,1},{4,6},{5,7},{6,4},{7,5},{8,10},{9,11},{10,... | collective-permute-start | bytes 1572872 | tf_op jit(solution)/shard_map/ppermute | solution.py:69
  18.7 79.4 %collective-permute-start = (bf16[512,512]{0,1:T(8,128)(2,1)}, bf16[512,512]{0,1:T(8,128)(2,1)}, u32[]{:S(2)}, u32[]{:S(2)}) collective-permute-start(bf16[512,512]{0,1:T(8,128)(2,1)} %fusion.24), channel_id=1, source_target_pairs={{0,1},{1,0},{2,3},{3,2},{4,5},{5,4},{6,7},{7,6},{8,9},{9,8},{10,11... | collective-permute-start | bytes 1572872 | tf_op jit(solution)/shard_map/ppermute | solution.py:69
  20.9 15.4 %copy-start.14 = (bf16[2,256,256]{2,1,0:T(8,128)(2,1)S(1)}, bf16[2,256,256]{2,1,0:T(8,128)(2,1)}, u32[]{:S(2)}) copy-start(bf16[2,256,256]{2,1,0:T(8,128)(2,1)} %param.31) | copy-start | bytes 786436
  23.1 13.3 %copy-start.5 = (bf16[2,256,512]{1,2,0:T(8,128)(2,1)S(1)}, bf16[2,256,512]{1,2,0:T(8,128)(2,1)}, u32[]{:S(2)}) copy-start(bf16[2,256,512]{1,2,0:T(8,128)(2,1)} %reshape.76) | copy-start | bytes 1572868
  33.6 33.7 %copy-start.2 = (bf16[4096,512]{1,0:T(8,128)(2,1)S(1)}, bf16[4096,512]{1,0:T(8,128)(2,1)}, u32[]{:S(2)}) copy-start(bf16[4096,512]{1,0:T(8,128)(2,1)} %copy-done.1) | copy-start | bytes 12582916
  33.6 33.7 %copy-start.3 = (bf16[8,512,512]{2,1,0:T(8,128)(2,1)S(1)}, bf16[8,512,512]{2,1,0:T(8,128)(2,1)}, u32[]{:S(2)}) copy-start(bf16[8,512,512]{2,1,0:T(8,128)(2,1)} %param.20) | copy-start | bytes 12582916
  35.4 25.8 %collective-permute-start.3 = (bf16[512,512]{1,0:T(8,128)(2,1)S(1)}, bf16[512,512]{1,0:T(8,128)(2,1)S(1)}, u32[]{:S(2)}, u32[]{:S(2)}) collective-permute-start(bf16[512,512]{1,0:T(8,128)(2,1)S(1)} %fusion.8), channel_id=1, source_target_pairs={{0,4},{1,5},{2,6},{3,7},{4,0},{5,1},{6,2},{7,3},{8,12},{9,13},{10,... | collective-permute-start | bytes 1572872 | tf_op jit(solution)/shard_map/ppermute | solution.py:69
  61.2 1.7 %copy-start.6 = (bf16[512,512]{1,0:T(8,128)(2,1)}, bf16[512,512]{1,0:T(8,128)(2,1)S(1)}, u32[]{:S(2)}) copy-start(bf16[512,512]{1,0:T(8,128)(2,1)S(1)} %collective-permute-done.3) | copy-start | bytes 1572868
  62.9 27.6 %collective-permute-start.4 = (bf16[512,512]{1,0:T(8,128)(2,1)S(1)}, bf16[512,512]{1,0:T(8,128)(2,1)S(1)}, u32[]{:S(2)}, u32[]{:S(2)}) collective-permute-start(bf16[512,512]{1,0:T(8,128)(2,1)S(1)} %fusion.10), channel_id=1, source_target_pairs={{0,8},{1,9},{2,10},{3,11},{4,12},{5,13},{6,14},{7,15},{8,0},{9,1},... | collective-permute-start | bytes 1572872 | tf_op jit(solution)/shard_map/ppermute | solution.py:69
  67.3 26.2 %copy-start.7 = (bf16[512,512]{1,0:T(8,128)(2,1)S(1)}, bf16[512,512]{1,0:T(8,128)(2,1)}, u32[]{:S(2)}) copy-start(bf16[512,512]{1,0:T(8,128)(2,1)} %copy-done.6) | copy-start | bytes 1572868
  103.0 1.9 %copy-start.10 = (bf16[8,128,256]{2,1,0:T(8,128)(2,1)S(1)}, bf16[8,128,256]{2,1,0:T(8,128)(2,1)}, u32[]{:S(2)}) copy-start(bf16[8,128,256]{2,1,0:T(8,128)(2,1)} %param.24) | copy-start | bytes 1572868
  104.9 2.3 %copy-start.15 = (bf16[8,128,128]{2,1,0:T(8,128)(2,1)S(1)}, bf16[8,128,128]{2,1,0:T(8,128)(2,1)}, u32[]{:S(2)}) copy-start(bf16[8,128,128]{2,1,0:T(8,128)(2,1)} %param.25) | copy-start | bytes 786436
where the time goes:
time: 117 us; the launch traced here: 116 us
  waiting for transfers between devices  50.6 us (43%)
  matrix products  41.7 us (36%)
  starting transfers between devices  10.4 us (9%)
  local copies, waits for them, and re-layouts  7.12 us (6%)
  other arithmetic  6.34 us (5%)
    ppermute x4, waiting for transfers between devices, body(): sib_x = lax.ppermute(node_x, 'tree', pair_list)  48.4 us
    dot_general x1, matrix products, body(): jnp.einsum('lmk,lkc->lmc', u_leaf, y_skel, preferred_element_type=jnp.flo...  9.25 us
    dot_general x3, matrix products, body(): jnp.dot(r_here, y_node, preferred_element_type=jnp.float32)  7.53 us
    dot_general x1, matrix products, body(): jnp.einsum('lmj,ljc->lmc', d_near, x_leaf, preferred_element_type=jnp.flo...  5.74 us
    ppermute x4, starting transfers between devices, body(): sib_x = lax.ppermute(node_x, 'tree', pair_list)  5.68 us
    ppermute x1, starting transfers between devices, body(): theirs = lax.ppermute(own_part, 'tree', pair_list)  4.77 us
    convert_element_type x1, other arithmetic, body(): x_leaf = x_loc.astype(jnp.bfloat16).reshape(leaves_dev, leaf_size, rhs_cols)  4.07 us
    dot_general x2, matrix products, body(): jnp.einsum('kq,kc->qc', pick_node(w_top, 2 ** level - 4 + sib_idx), sib_x...  3.38 us
  transfers between devices with their start and end apart: 5, of which 4 were waited for; matrix products, arithmetic and copies ran while one was open for 22% of the time, Pallas kernels for 0%

commit v1 on v0

v1 whole, which is shorter than its diff:
```python
import functools
import math

import jax
import jax.numpy as jnp
from jax import lax
from jax.experimental import pallas as pl
from jax.experimental.pallas import tpu as pltpu
from jax.sharding import PartitionSpec as P

MESH = pl.DeviceIdType.MESH
F32 = jnp.float32
BF16 = jnp.bfloat16
VMEM_ALL = pl.BlockSpec(memory_space=pltpu.VMEM)
HBM_ALL = pl.BlockSpec(memory_space=pl.ANY)


def log_two(count):
    return int(math.log2(count) + 0.5)


def mm(lhs, rhs, lhs_dim, rhs_dim):
    return lax.dot_general(lhs, rhs, (((lhs_dim,), (rhs_dim,)), ((), ())), preferred_element_type=F32)


def up_kernel(devs, x_hbm, d_hbm, v_hbm, w0_hbm, b0_hbm, w1_hbm, b1_hbm, w2_hbm, b2_hbm, wu_hbm, bu_hbm, ru_hbm, wt_hbm, rt_hbm, bt_hbm,
              y_dev, near, g0, g1, g2,
              xf, xb, d, v, w0, b0, w1, b1, w2, b2, wu, bu, ru, wt, rt, bt, xh0, xh1, xh2, xt, xsib, xchip, xall, x2, x1, x1_sib, y_out, y_all,
              x_sem, d_sem, v_sem, w_sem, wsib_sem, swap_send, swap_recv, out_send, out_recv, top_send, top_recv, back_send, back_recv, pair_send, pair_recv):
    me = lax.axis_index('tree')
    chips = devs // 2
    half_chips = chips // 2
    core = lax.rem(me, 2)
    chip = me // 2
    other = 1 - core
    partner = chip * 2 + other
    leaves, leaf_size, cols = xf.shape
    part = cols // devs
    half = cols // 2
    my_half = chip // half_chips

    barrier = pltpu.get_barrier_semaphore()
    for step in range(1, devs):
        pl.semaphore_signal(barrier, inc=1, device_id={'tree': lax.rem(me + step, devs)}, device_id_type=MESH)

    def load_x(i):
        return pltpu.make_async_copy(x_hbm.at[pl.ds(i * leaf_size, leaf_size)], xf.at[i], x_sem.at[i])

    def load_d(i):
        return pltpu.make_async_copy(d_hbm.at[i], d.at[i], d_sem.at[i])

    def load_v(i):
        return pltpu.make_async_copy(v_hbm.at[i], v.at[i], v_sem.at[i])

    def top_slices(hbm, vmem, first, base):
        out = []
        at = 0
        for level in range(first, log_two(devs)):
            count = 2 ** (level - 1)
            start = 2 ** level - 2 ** first + core * count
            out.append(pltpu.make_async_copy(hbm.at[pl.ds(start, count)], vmem.at[pl.ds(at, count)], w_sem.at[base + level]))
            at += count
        return out

    copies = {}
    for k, (name, hbm, vmem) in enumerate([('w0', w0_hbm, w0), ('w1', w1_hbm, w1), ('w2', w2_hbm, w2), ('wu', wu_hbm.at[0], wu.at[0]), ('bu', bu_hbm.at[0], bu), ('ru', ru_hbm.at[0], ru), ('b0', b0_hbm, b0), ('b1', b1_hbm, b1), ('b2', b2_hbm, b2)]):
        copies[name] = pltpu.make_async_copy(hbm, vmem, w_sem.at[k])
    depth = log_two(devs)
    wt_copies = top_slices(wt_hbm, wt, 2, 9)
    rt_copies = top_slices(rt_hbm, rt, 2, 9 + depth)
    bt_copies = top_slices(bt_hbm, bt, 1, 9 + 2 * depth)

    ahead = 4
    for i in range(ahead):
        load_v(i).start()
        load_x(i).start()
    copies['w0'].start()
    copies['w1'].start()

    wsib = pltpu.make_async_remote_copy(wu.at[0], wu.at[1], wsib_sem.at[0], wsib_sem.at[1], device_id={'tree': partner}, device_id_type=MESH)

    for i in range(leaves):
        load_v(i).wait()
        load_x(i).wait()
        if i + ahead < leaves:
            load_v(i + ahead).start()
            load_x(i + ahead).start()
        if i == 1:
            copies['wu'].start()
            copies['w2'].start()
        if i == ahead - 1:
            for name in ('bu', 'b0', 'b1', 'b2'):
                copies[name].start()
            for j in range(leaves):
                load_d(j).start()
            for copy in wt_copies + bt_copies + rt_copies:
                copy.start()
            copies['ru'].start()
        xb[i] = xf[i].astype(BF16)
        xh0[i] = mm(v[i], xb[i], 0, 0).astype(BF16)
        if i % 2 == 1:
            n = i // 2
            if n == 0:
                copies['w0'].wait()
            xh1[n] = (mm(w0[2 * n], xh0[2 * n], 0, 0) + mm(w0[2 * n + 1], xh0[2 * n + 1], 0, 0)).astype(BF16)
        if i % 4 == 3:
            n = i // 4
            if n == 0:
                copies['w1'].wait()
                copies['wu'].wait()
                pl.semaphore_wait(barrier, devs - 1)
                wsib.start()
            xh2[n] = (mm(w1[2 * n], xh1[2 * n], 0, 0) + mm(w1[2 * n + 1], xh1[2 * n + 1], 0, 0)).astype(BF16)
    copies['w2'].wait()

    swaps = []
    for k, side in enumerate((other, core)):
        window = pl.ds(pl.multiple_of(side * half, half), half)
        xt[side] = (mm(xh2[0, :, window], w2[0], 0, 0) + mm(xh2[1, :, window], w2[1], 0, 0)).astype(BF16)
        swaps.append(pltpu.make_async_remote_copy(xt.at[side], xsib.at[side], swap_send.at[k], swap_recv.at[k], device_id={'tree': partner}, device_id_type=MESH))
        swaps[-1].start()
    got = [pltpu.make_async_remote_copy(xt.at[core], xsib.at[core], swap_send.at[0], swap_recv.at[0], device_id={'tree': partner}, device_id_type=MESH),
           pltpu.make_async_remote_copy(xt.at[other], xsib.at[other], swap_send.at[1], swap_recv.at[1], device_id={'tree': partner}, device_id_type=MESH)]

    def near_leaf(i):
        load_d(i).wait()
        near[i] = mm(d[i], xb[i], 1, 0)

    near_leaf(0)
    near_leaf(1)
    wsib.wait()
    got[0].wait_recv()
    merged = (mm(xt[core], wu[0], 1, 0) + mm(xsib[core], wu[1], 1, 0)).astype(BF16)
    xchip[...] = merged.reshape(xchip.shape)

    def out_copy(step):
        dest = lax.rem(chip + step, chips)
        slot = lax.rem(chip, half_chips)
        return pltpu.make_async_remote_copy(xchip.at[dest], xall.at[slot, core], out_send.at[step], out_recv.at[slot, core], device_id={'tree': dest * 2 + my_half}, device_id_type=MESH)

    far_first = [half_chips]
    for step in range(half_chips - 1, 0, -1):
        far_first += [step, chips - step]
    for step in far_first:
        out_copy(step).start()

    @pl.when(core != my_half)
    def _():
        out_copy(0).start()

    @pl.when(core == my_half)
    def _():
        xall[lax.rem(chip, half_chips), core] = xchip[chip]

    for i in range(2, leaves):
        near_leaf(i)
    copies['b0'].wait()
    copies['b1'].wait()
    copies['b2'].wait()
    for n in range(leaves):
        g0[n] = mm(b0[n], xh0[n ^ 1], 1, 0)
    for n in range(leaves // 2):
        g1[n] = mm(b1[n], xh1[n ^ 1], 1, 0)
    for n in range(leaves // 4):
        g2[n] = mm(b2[n], xh2[n ^ 1], 1, 0)
    got[1].wait_recv()
    copies['bu'].wait()
    copies['ru'].wait()
    g_dev = mm(bu[...], xsib[...].reshape(cols, -1), 1, 1)
    for copy in wt_copies + bt_copies + rt_copies:
        copy.wait()

    for n in range(half_chips):
        for c in range(2):
            local = jnp.logical_and(core * half_chips + n == chip, core == c)
            landed = pltpu.make_async_remote_copy(xchip.at[0], xall.at[n, c], out_send.at[0], out_recv.at[n, c], device_id={'tree': partner}, device_id_type=MESH)

            @pl.when(jnp.logical_not(local))
            def _():
                landed.wait_recv()

    mine = 2 * part
    levels = [[xall[n].reshape(mine, -1) for n in range(half_chips)]]
    at = [0]
    for level in range(depth - 1, 1, -1):
        at.append(0)
    w_at = {}
    pos = 0
    for level in range(2, depth):
        w_at[level] = pos
        pos += 2 ** (level - 1)
    b_at = {}
    pos = 0
    for level in range(1, depth):
        b_at[level] = pos
        pos += 2 ** (level - 1)
    for level in range(depth - 1, 1, -1):
        below = levels[-1]
        base = w_at[level]
        levels.append([(mm(below[2 * q], wt[base + 2 * q], 1, 0) + mm(below[2 * q + 1], wt[base + 2 * q + 1], 1, 0)).astype(BF16) for q in range(len(below) // 2)])
    x1[...] = levels[-1][0]
    top_swap = pltpu.make_async_remote_copy(x1, x1_sib, top_send.at[0], top_recv.at[0], device_id={'tree': partner}, device_id_type=MESH)
    top_swap.start()
    g_top = {}
    for level in range(depth - 1, 1, -1):
        nodes = levels[depth - 1 - level]
        g_top[level] = [mm(nodes[n ^ 1], bt[b_at[level] + n], 1, 1) for n in range(len(nodes))]
    top_swap.wait()
    y_top = [mm(x1_sib[...], bt[b_at[1]], 1, 1).astype(BF16)]
    for level in range(2, depth):
        y_top = [(g_top[level][n] + mm(y_top[n // 2], rt[w_at[level] + n], 1, 1)).astype(BF16) for n in range(len(g_top[level]))]
    for n in range(half_chips):
        y_out[n] = y_top[n].reshape(y_out.shape[1:])

    def back_copy(n, c):
        dest = core * half_chips + n
        return pltpu.make_async_remote_copy(y_out.at[n, c], y_all.at[c, chip], back_send.at[n, c], back_recv.at[chip], device_id={'tree': dest * 2 + c}, device_id_type=MESH)

    for n in range(half_chips):
        for c in range(2):
            local = jnp.logical_and(core * half_chips + n == chip, core == c)

            @pl.when(jnp.logical_not(local))
            def _():
                back_copy(n, c).start()

            @pl.when(local)
            def _():
                y_all[c, chip] = y_out[n, c]

    for j in range(chips):
        landed = pltpu.make_async_remote_copy(y_out.at[0, 0], y_all.at[core, j], back_send.at[0, 0], back_recv.at[j], device_id={'tree': partner}, device_id_type=MESH)

        @pl.when(jnp.logical_or(j != chip, core != my_half))
        def _():
            landed.wait_recv()

    pair = pltpu.make_async_remote_copy(y_all.at[core], y_all.at[core], pair_send.at[0], pair_recv.at[0], device_id={'tree': partner}, device_id_type=MESH)
    pair.start()
    pltpu.make_async_remote_copy(y_all.at[other], y_all.at[other], pair_send.at[0], pair_recv.at[0], device_id={'tree': partner}, device_id_type=MESH).wait_recv()
    y_dev[...] = (g_dev + mm(ru[...], y_all[...].reshape(cols, -1), 1, 1)).astype(BF16)

    for swap in swaps:
        swap.wait_send()
    for step in far_first:
        out_copy(step).wait_send()

    @pl.when(core != my_half)
    def _():
        out_copy(0).wait_send()

    for n in range(half_chips):
        for c in range(2):
            local = jnp.logical_and(core * half_chips + n == chip, core == c)

            @pl.when(jnp.logical_not(local))
            def _():
                back_copy(n, c).wait_send()

    pair.wait_send()


def down_kernel(y_dev, near, g0, g1, g2, r0, r1, r2, u, out_hbm, y2, y1, stage, out_sem):
    leaves, leaf_size, cols = stage.shape

    def store(i):
        return pltpu.make_async_copy(stage.at[i], out_hbm.at[pl.ds(i * leaf_size, leaf_size)], out_sem.at[i])

    for i in range(leaves):
        if i % 4 == 0:
            y2[i // 4] = (g2[i // 4] + mm(r2[i // 4], y_dev[...], 1, 0)).astype(BF16)
        if i % 2 == 0:
            y1[i // 2] = (g1[i // 2] + mm(r1[i // 2], y2[i // 4], 1, 0)).astype(BF16)
        y_leaf = (g0[i] + mm(r0[i], y1[i // 2], 1, 0)).astype(BF16)
        stage[i] = near[i] + mm(u[i], y_leaf, 1, 0)
        store(i).start()
    for i in range(leaves):
        store(i).wait()


def solution(mesh):
    devs = mesh.shape['tree']
    rows_spec = P(('batch', 'tree'), None)
    tree_spec = P('tree', None, None)
    full_spec = P(None, None, None)

    def body(x_loc, d_near, u_leaf, v_leaf, w_h0, r_h0, b_h0, w_h1, r_h1, b_h1, w_h2, r_h2, b_h2, w_upper, r_upper, b_upper, w_top, r_top, b_top):
        leaves, leaf_size, rank0 = u_leaf.shape
        cols = x_loc.shape[1]
        rank1 = w_h0.shape[2]
        rank2 = w_h1.shape[2]
        rank3 = w_h2.shape[2]
        chips = devs // 2
        part = cols // devs
        half = cols // 2
        depth = log_two(devs)
        sds = jax.ShapeDtypeStruct
        dma = pltpu.SemaphoreType.DMA
        vmem = pltpu.VMEM
        outs = [sds((rank3, cols), BF16), sds((leaves, leaf_size, cols), F32), sds((leaves, rank0, cols), F32), sds((leaves // 2, rank1, cols), F32), sds((leaves // 4, rank2, cols), F32)]
        half_nodes = chips - 2
        scratch = [
            vmem((leaves, leaf_size, cols), F32), vmem((leaves, leaf_size, cols), BF16), vmem(d_near.shape[:0] + (leaves, leaf_size, leaf_size), BF16),
            vmem((leaves, leaf_size, rank0), BF16),
            vmem((leaves, rank0, rank1), BF16), vmem((leaves, rank0, rank0), BF16),
            vmem((leaves // 2, rank1, rank2), BF16), vmem((leaves // 2, rank1, rank1), BF16),
            vmem((leaves // 4, rank2, rank3), BF16), vmem((leaves // 4, rank2, rank2), BF16),
            vmem((2, rank3, rank3), BF16), vmem((rank3, rank3), BF16), vmem((rank3, rank3), BF16),
            vmem((half_nodes, rank3, rank3), BF16), vmem((half_nodes, rank3, rank3), BF16), vmem((half_nodes + 1, rank3, rank3), BF16),
            vmem((leaves, rank0, cols), BF16), vmem((leaves // 2, rank1, cols), BF16), vmem((leaves // 4, rank2, cols), BF16),
            vmem((2, half, rank3), BF16), vmem((2, half, rank3), BF16),
            vmem((chips, part, rank3), BF16), vmem((chips // 2, 2, part, rank3), BF16),
            vmem((2, 2 * part, rank3), BF16), vmem((2 * part, rank3), BF16), vmem((2 * part, rank3), BF16),
            vmem((chips // 2, 2, part, rank3), BF16), vmem((2, chips, part, rank3), BF16),
            dma((leaves,)), dma((leaves,)), dma((leaves,)), dma((9 + 3 * depth,)), dma((2,)),
            dma((2,)), dma((2,)), dma((chips,)), dma((chips // 2, 2)), dma((1,)), dma((1,)), dma((chips // 2, 2)), dma((chips,)), dma((1,)), dma((1,)),
        ]
        y_dev, near, g0, g1, g2 = pl.pallas_call(
            functools.partial(up_kernel, devs),
            out_shape=outs,
            in_specs=[HBM_ALL] * 15,
            out_specs=[VMEM_ALL] * 5,
            scratch_shapes=scratch,
            compiler_params=pltpu.CompilerParams(collective_id=0, has_side_effects=True, vmem_limit_bytes=60 * 2 ** 20),
            name='up_top',
        )(x_loc, d_near, v_leaf, w_h0, b_h0, w_h1, b_h1, w_h2, b_h2, w_upper, b_upper, r_upper, w_top, r_top, b_top)
        return pl.pallas_call(
            down_kernel,
            out_shape=sds(x_loc.shape, F32),
            in_specs=[VMEM_ALL] * 9,
            out_specs=HBM_ALL,
            scratch_shapes=[vmem((leaves // 4, rank2, cols), BF16), vmem((leaves // 2, rank1, cols), BF16), vmem((leaves, leaf_size, cols), F32), dma((leaves,))],
            compiler_params=pltpu.CompilerParams(vmem_limit_bytes=60 * 2 ** 20),
            name='down_out',
        )(y_dev, near, g0, g1, g2, r_h0, r_h1, r_h2, u_leaf)

    return jax.shard_map(body, mesh=mesh, in_specs=(rows_spec,) + (tree_spec,) * 15 + (full_spec,) * 3, out_specs=rows_spec, check_vma=False)
```

time: 117 us -> 51.4 us (0.44)
  Pallas kernels: 0 us -> 50.8 us
  waiting for transfers between devices: 50.6 us -> 0 us
  matrix products: 41.7 us -> 0 us
  starting transfers between devices: 10.4 us -> 0 us
  local copies, waits for them, and re-layouts: 7.12 us -> 0 us
  other arithmetic: 6.34 us -> 0 us
    pallas_call x0 -> x2, Pallas kernels: none -> 50.8 us  [the longest x1 40.1 us: body(): pl.pallas_call(functools.partial(up_kernel, devs), out_shape=outs, in_spe...]
    ppermute x5 -> x0, waiting for transfers between devices: 50.6 us -> none  [the longest x4 48.4 us: body(): sib_x = lax.ppermute(node_x, 'tree', pair_list)]
    dot_general x19 -> x0, matrix products: 41.7 us -> none  [the longest x1 9.25 us: body(): jnp.einsum('lmk,lkc->lmc', u_leaf, y_skel, preferred_element_type=jnp.flo...]
    ppermute x5 -> x0, starting transfers between devices: 10.4 us -> none  [the longest x4 5.68 us: body(): sib_x = lax.ppermute(node_x, 'tree', pair_list)]
    convert_element_type x5 -> x0, other arithmetic: 6.34 us -> none  [the longest x1 4.07 us: body(): x_leaf = x_loc.astype(jnp.bfloat16).reshape(leaves_dev, leaf_size, rhs_cols)]
    reshape x2 -> x0, local copies, waits for them, and re-layouts: 3.73 us -> none  [the longest x1 1.9 us: couple_local(): swapped = jnp.flip(pairs, axis=1).reshape(x_level.shape)]
    rev x2 -> x0, local copies, waits for them, and re-layouts: 2.11 us -> none  [couple_local(): swapped = jnp.flip(pairs, axis=1).reshape(x_level.shape)]
    unnamed x32 -> x0, local copies, waits for them, and re-layouts: 1.28 us -> none
  transfers between devices with their start and end apart: 5 -> 0, of which waited for: 4 -> 0; matrix products, arithmetic and copies ran while one was open for 22% -> 0% of each run, Pallas kernels for 0% -> 0%
where the time goes in v1:
time: 51.4 us; the launch traced here: 50.8 us
  Pallas kernels  50.8 us (99%)
    pallas_call x1, Pallas kernels, body(): pl.pallas_call(functools.partial(up_kernel, devs), out_shape=outs, in_spe...  40.1 us
    pallas_call x1, Pallas kernels, body(): pl.pallas_call(down_kernel, out_shape=sds(x_loc.shape, F32), in_specs=[VM...  10.7 us

profile of v1, /device:TPU:21, one launch (start us, length us, event | category | flops | bytes accessed | tf_op | source)
XLA Modules:
  0.0 50.8 jit_solution(10691997832913129871)
XLA Ops:
  0.0 40.1 %up_top.1 = (bf16[512,512]{1,0:T(8,128)(2,1)}, f32[8,512,512]{2,1,0:T(8,128)}, f32[8,128,512]{2,1,0:T(8,128)}, f32[4,256,512]{2,1,0:T(8,128)}, f32[2,256,512]{2,1,0:T(8,128)}) custom-call(f32[4096,512]{1,0:T(8,128)} %x_hbm.1, bf16[8,512,512]{2,1,0:T(8,128)(2,1)} %d_hbm.1, bf16[8,512,128]{2,1,0:T(8,128)(2,1)} %v_hbm.1, bf16[8,128,256]{2,1,0:T(8,128)(2,1)} %w0_hbm.1, ...), custom_call_target="tpu_custom_call" | custom-call | tf_op jit(solution)/shard_map/up_top/pallas_call | solution.py:318
  40.1 10.7 %down_out.1 = f32[4096,512]{1,0:T(8,128)} custom-call(bf16[512,512]{1,0:T(8,128)(2,1)} %get-tuple-element.10.y_dev, f32[8,512,512]{2,1,0:T(8,128)} %get-tuple-element.11.near, f32[8,128,512]{2,1,0:T(8,128)} %get-tuple-element.12.g0, f32[4,256,512]{2,1,0:T(8,128)} %get-tuple-element.13.g1, f32[2,256,512]{2,1,0:T(8,128)} %get-tuple-element.14.g2, ...), custom_call_target="tpu_custom_call" | custom-call | tf_op jit(solution)/shard_map/down_out/pallas_call | solution.py:327

commit v2 on v1

--- a/solution.py
+++ b/solution.py
@@ -12,7 +12,7 @@
 F32 = jnp.float32
 BF16 = jnp.bfloat16
 VMEM_ALL = pl.BlockSpec(memory_space=pltpu.VMEM)
-HBM_ALL = pl.BlockSpec(memory_space=pl.ANY)
+HBM_ALL = pl.BlockSpec(memory_space=pltpu.HBM)
 
 
 def log_two(count):
@@ -25,7 +25,7 @@
 
 def up_kernel(devs, x_hbm, d_hbm, v_hbm, w0_hbm, b0_hbm, w1_hbm, b1_hbm, w2_hbm, b2_hbm, wu_hbm, bu_hbm, ru_hbm, wt_hbm, rt_hbm, bt_hbm,
               y_dev, near, g0, g1, g2,
-              xf, xb, d, v, w0, b0, w1, b1, w2, b2, wu, bu, ru, wt, rt, bt, xh0, xh1, xh2, xt, xsib, xchip, xall, x2, x1, x1_sib, y_out, y_all,
+              xb, d, v, w0, b0, w1, b1, w2, b2, wu, bu, ru, wt, rt, bt, xh0, xh1, xh2, xt, xsib, xchip, xall, x2, x1, x1_sib, y_out, y_all,
               x_sem, d_sem, v_sem, w_sem, wsib_sem, swap_send, swap_recv, out_send, out_recv, top_send, top_recv, back_send, back_recv, pair_send, pair_recv):
     me = lax.axis_index('tree')
     chips = devs // 2
@@ -34,7 +34,7 @@
     chip = me // 2
     other = 1 - core
     partner = chip * 2 + other
-    leaves, leaf_size, cols = xf.shape
+    leaves, leaf_size, cols = xb.shape
     part = cols // devs
     half = cols // 2
     my_half = chip // half_chips
@@ -44,7 +44,7 @@
         pl.semaphore_signal(barrier, inc=1, device_id={'tree': lax.rem(me + step, devs)}, device_id_type=MESH)
 
     def load_x(i):
-        return pltpu.make_async_copy(x_hbm.at[pl.ds(i * leaf_size, leaf_size)], xf.at[i], x_sem.at[i])
+        return pltpu.make_async_copy(x_hbm.at[pl.ds(i * leaf_size, leaf_size)], near.at[i], x_sem.at[i])
 
     def load_d(i):
         return pltpu.make_async_copy(d_hbm.at[i], d.at[i], d_sem.at[i])
@@ -96,7 +96,7 @@
             for copy in wt_copies + bt_copies + rt_copies:
                 copy.start()
             copies['ru'].start()
-        xb[i] = xf[i].astype(BF16)
+        xb[i] = near[i].astype(BF16)
         xh0[i] = mm(v[i], xb[i], 0, 0).astype(BF16)
         if i % 2 == 1:
             n = i // 2
@@ -297,10 +297,10 @@
         sds = jax.ShapeDtypeStruct
         dma = pltpu.SemaphoreType.DMA
         vmem = pltpu.VMEM
-        outs = [sds((rank3, cols), BF16), sds((leaves, leaf_size, cols), F32), sds((leaves, rank0, cols), F32), sds((leaves // 2, rank1, cols), F32), sds((leaves // 4, rank2, cols), F32)]
+        outs = [vmem((rank3, cols), BF16), vmem((leaves, leaf_size, cols), F32), vmem((leaves, rank0, cols), F32), vmem((leaves // 2, rank1, cols), F32), vmem((leaves // 4, rank2, cols), F32)]
         half_nodes = chips - 2
         scratch = [
-            vmem((leaves, leaf_size, cols), F32), vmem((leaves, leaf_size, cols), BF16), vmem(d_near.shape[:0] + (leaves, leaf_size, leaf_size), BF16),
+            vmem((leaves, leaf_size, cols), BF16), vmem((leaves, leaf_size, leaf_size), BF16),
             vmem((leaves, leaf_size, rank0), BF16),
             vmem((leaves, rank0, rank1), BF16), vmem((leaves, rank0, rank0), BF16),
             vmem((leaves // 2, rank1, rank2), BF16), vmem((leaves // 2, rank1, rank1), BF16),
@@ -321,17 +321,17 @@
             in_specs=[HBM_ALL] * 15,
             out_specs=[VMEM_ALL] * 5,
             scratch_shapes=scratch,
-            compiler_params=pltpu.CompilerParams(collective_id=0, has_side_effects=True, vmem_limit_bytes=60 * 2 ** 20),
+            compiler_params=pltpu.CompilerParams(collective_id=0, has_side_effects=True, vmem_limit_bytes=38 * 2 ** 20),
             name='up_top',
-        )(x_loc, d_near, v_leaf, w_h0, b_h0, w_h1, b_h1, w_h2, b_h2, w_upper, b_upper, r_upper, w_top, r_top, b_top)
+        )(*[pltpu.with_memory_space_constraint(a, pltpu.HBM) for a in (x_loc, d_near, v_leaf, w_h0, b_h0, w_h1, b_h1, w_h2, b_h2, w_upper, b_upper, r_upper, w_top, r_top, b_top)])
         return pl.pallas_call(
             down_kernel,
             out_shape=sds(x_loc.shape, F32),
             in_specs=[VMEM_ALL] * 9,
             out_specs=HBM_ALL,
             scratch_shapes=[vmem((leaves // 4, rank2, cols), BF16), vmem((leaves // 2, rank1, cols), BF16), vmem((leaves, leaf_size, cols), F32), dma((leaves,))],
-            compiler_params=pltpu.CompilerParams(vmem_limit_bytes=60 * 2 ** 20),
+            compiler_params=pltpu.CompilerParams(vmem_limit_bytes=14 * 2 ** 20),
             name='down_out',
-        )(y_dev, near, g0, g1, g2, r_h0, r_h1, r_h2, u_leaf)
+        )(*[pltpu.with_memory_space_constraint(a, pltpu.VMEM) for a in (y_dev, near, g0, g1, g2, r_h0, r_h1, r_h2, u_leaf)])
 
     return jax.shard_map(body, mesh=mesh, in_specs=(rows_spec,) + (tree_spec,) * 15 + (full_spec,) * 3, out_specs=rows_spec, check_vma=False)

time: 51.4 us -> 41.2 us (0.80)
  Pallas kernels: 50.8 us -> 40.6 us
    pallas_call x1, Pallas kernels: 10.7 us -> 4.94 us  [body(): pl.pallas_call(down_kernel, out_shape=sds(x_loc.shape, F32), in_specs=[VM...]
    pallas_call x1, Pallas kernels: 40.1 us -> 35.7 us  [body(): pl.pallas_call(functools.partial(up_kernel, devs), out_shape=outs, in_spe...]
where the time goes in v2:
time: 41.2 us; the launch traced here: 40.7 us
  Pallas kernels  40.6 us (99%)
    pallas_call x1, Pallas kernels, body(): pl.pallas_call(functools.partial(up_kernel, devs), out_shape=outs, in_spe...  35.7 us
    pallas_call x1, Pallas kernels, body(): pl.pallas_call(down_kernel, out_shape=sds(x_loc.shape, F32), in_specs=[VM...  4.94 us

profile of v2, /device:TPU:21, one launch (start us, length us, event | category | flops | bytes accessed | tf_op | source)
XLA Modules:
  0.0 40.7 jit_solution(149082820919189324)
XLA Ops:
  0.0 0.0 copy-start.3
  0.0 0.0 copy-start.2
  0.0 0.0 copy-start.1
  0.0 0.0 copy-start
  0.0 35.7 %up_top.1 = (bf16[512,512]{1,0:T(8,128)(2,1)S(1)}, f32[8,512,512]{2,1,0:T(8,128)S(1)}, f32[8,128,512]{2,1,0:T(8,128)S(1)}, f32[4,256,512]{2,1,0:T(8,128)S(1)}, f32[2,256,512]{2,1,0:T(8,128)S(1)}) custom-call(f32[4096,512]{1,0:T(8,128)} %x_hbm.1, bf16[8,512,512]{2,1,0:T(8,128)(2,1)} %d_hbm.1, bf16[8,512,128]{2,1,0:T(8,128)(2,1)} %v_hbm.1, ...), custom_call_target="tpu_custom_call" | custom-call | tf_op jit(solution)/shard_map/up_top/pallas_call | solution.py:318
  35.7 0.0 copy-done.3
  35.7 0.0 copy-done.2
  35.7 0.0 copy-done.1
  35.7 0.0 copy-done
  35.7 4.9 %down_out.1 = f32[4096,512]{1,0:T(8,128)} custom-call(bf16[512,512]{1,0:T(8,128)(2,1)S(1)} %get-tuple-element.10.y_dev, f32[8,512,512]{2,1,0:T(8,128)S(1)} %get-tuple-element.11.near, f32[8,128,512]{2,1,0:T(8,128)S(1)} %get-tuple-element.12.g0, f32[4,256,512]{2,1,0:T(8,128)S(1)} %get-tuple-element.13.g1, f32[2,256,512]{2,1,0:T(8,128)S(1)} %get-tuple-element.14.g2, ...), custom_call_target="tpu_custom_call" | custom-call | tf_op jit(solution)/shard_map/down_out/pallas_call | solution.py:327
Async XLA Ops:
  0.0 35.7 %copy-start.3 = (bf16[2,256,512]{2,1,0:T(8,128)(2,1)S(1)}, bf16[2,256,512]{2,1,0:T(8,128)(2,1)}, u32[]{:S(2)}) copy-start(bf16[2,256,512]{2,1,0:T(8,128)(2,1)} %r2.1) | copy-start | bytes 1572868
  0.0 35.7 %copy-start.2 = (bf16[4,256,256]{2,1,0:T(8,128)(2,1)S(1)}, bf16[4,256,256]{2,1,0:T(8,128)(2,1)}, u32[]{:S(2)}) copy-start(bf16[4,256,256]{2,1,0:T(8,128)(2,1)} %r1.1) | copy-start | bytes 1572868
  0.0 35.7 %copy-start.1 = (bf16[8,128,256]{2,1,0:T(8,128)(2,1)S(1)}, bf16[8,128,256]{2,1,0:T(8,128)(2,1)}, u32[]{:S(2)}) copy-start(bf16[8,128,256]{2,1,0:T(8,128)(2,1)} %r0.1) | copy-start | bytes 1572868
  0.0 35.7 %copy-start = (bf16[8,512,128]{2,1,0:T(8,128)(2,1)S(1)}, bf16[8,512,128]{2,1,0:T(8,128)(2,1)}, u32[]{:S(2)}) copy-start(bf16[8,512,128]{2,1,0:T(8,128)(2,1)} %u.1) | copy-start | bytes 3145732
